TPU v7x, 512 devices: a 4x2x32 block of a 4x8x32 slice. The times are simulated.
512 devices in a mesh: sweep: 2 (over y), row: 8 (over x, core), col: 32 (over z).
Axes of the slice: x: 4, y: 2, z: 32, core: 2. Of those that a mesh axis runs over, the one named last changes fastest.
The devices are a block of a 4x8x32 slice.
Arguments:
- tokens: bfloat16 [1280, 4096], P(('sweep', 'col'), 'row'), parts along dimension 0, may hold values from -6 to 6
- w_gate: bfloat16 [4096, 14336], P('row', 'col'), may hold values from -0.09375 to 0.09375
- w_up: bfloat16 [4096, 14336], P('row', 'col'), may hold values from -0.09375 to 0.09375
- w_down: bfloat16 [14336, 4096], P('col', 'row'), may hold values from -0.046875 to 0.046875
- cotangent: bfloat16 [1280, 4096], P(('sweep', 'col'), 'row'), parts along dimension 0, may hold values from -6 to 6
- step_rate: float32 [2], P('sweep'), parts along dimension 0, may hold values from 0.05 to 0.3
Outputs:
- out_rows: bfloat16 [1280, 4096], P(('sweep', 'col'), 'row'), parts along dimension 0
- grad_in: bfloat16 [1280, 4096], P(('sweep', 'col'), 'row'), parts along dimension 0
- step_gate: bfloat16 [8192, 14336], P(('sweep', 'row'), 'col'), parts along dimension 0
- step_up: bfloat16 [8192, 14336], P(('sweep', 'row'), 'col'), parts along dimension 0
- step_down: bfloat16 [28672, 4096], P(('sweep', 'col'), 'row'), parts along dimension 0
There are 2 independent parts, one for each index of `sweep`. A program takes and returns all parts, laid end to end along the dimension named above; an argument that names none is the same for every part. Nothing has to cross between parts.
All inputs are finite; a program needn't handle non-finite values.
Results may differ from a plain program's by a relative error of at most 0.0049.
Values may be sent and summed in bfloat16 or wider, within the bound.
No kernel may reach another device: no remote copies, remote signals or barrier semaphores. Data moves between devices by JAX's collectives and lax.ppermute only.
A program may use at most 64 MiB of HBM per device.

v0:
```python
import jax
import jax.numpy as jnp
from jax import lax
from jax.sharding import PartitionSpec as P


def cut_along(value, dim, count):
    before, after = (value.shape[:dim], value.shape[dim + 1 :])
    return jnp.moveaxis(value.reshape(*before, count, -1, *after), dim, 0)


def summed_on_arrival(value, axis, dim):
    count = lax.axis_size(axis)
    parts = lax.all_to_all(cut_along(value, dim, count), axis, 0, 0, tiled=True)
    return jnp.sum(parts, axis=0)


def swiglu_back(back_hidden, gate_val, up_val):
    gate_sig = jax.nn.sigmoid(gate_val)
    activation = gate_val * gate_sig
    back_gate = (back_hidden * up_val * gate_sig * (1.0 + gate_val * (1.0 - gate_sig))).astype(
        jnp.bfloat16
    )
    back_up = (back_hidden * activation).astype(jnp.bfloat16)
    return (back_gate, back_up)


def forward_hidden(gate_val, up_val):
    gate_sig = jax.nn.sigmoid(gate_val)
    return (gate_val * gate_sig * up_val).astype(jnp.bfloat16)


def contract_last(left, right):
    return lax.dot_general(
        left, right, (((1,), (1,)), ((), ())), preferred_element_type=jnp.float32
    )


def contract_first(left, right):
    return lax.dot_general(
        left, right, (((0,), (0,)), ((), ())), preferred_element_type=jnp.float32
    )


def local(tokens, w_gate, w_up, w_down, cotangent, step_rate):
    tokens_all = lax.all_gather(tokens, "col", axis=0, tiled=True)
    hidden_width = w_gate.shape[1]
    w_both = jnp.concatenate([w_gate, w_up], axis=1)
    picked = tokens_all
    summed = summed_on_arrival(
        jnp.dot(picked, w_both, preferred_element_type=jnp.float32), "row", 0
    )
    gate_val = summed[:, :hidden_width]
    up_val = summed[:, hidden_width:]
    hidden = forward_hidden(gate_val, up_val)
    hidden_all = lax.all_gather(hidden, "row", axis=0, tiled=True)
    picked = hidden_all
    branch_out = lax.psum_scatter(
        jnp.dot(picked, w_down, preferred_element_type=jnp.float32),
        "col",
        scatter_dimension=0,
        tiled=True,
    )
    out_rows = (tokens.astype(jnp.float32) + branch_out).astype(jnp.bfloat16)
    cotangent_all = lax.all_gather(cotangent, "col", axis=0, tiled=True)
    picked = cotangent_all
    back_hidden = lax.psum_scatter(
        contract_last(picked, w_down), "row", scatter_dimension=0, tiled=True
    )
    back_gate, back_up = swiglu_back(back_hidden, gate_val, up_val)
    gate_grad_all, up_grad_all = (
        lax.all_gather(back_gate, "row", axis=0, tiled=True),
        lax.all_gather(back_up, "row", axis=0, tiled=True),
    )
    grads_all = jnp.concatenate([gate_grad_all, up_grad_all], axis=1)
    picked = grads_all
    input_sums = lax.psum_scatter(
        contract_last(picked, w_both), "col", scatter_dimension=0, tiled=True
    )
    grad_in = (cotangent.astype(jnp.float32) + input_sums).astype(jnp.bfloat16)
    factor = -step_rate[0]
    weight_grads = contract_first(tokens_all, grads_all)
    step_gate = (factor * weight_grads[:, :hidden_width]).astype(jnp.bfloat16)
    step_up = (factor * weight_grads[:, hidden_width:]).astype(jnp.bfloat16)
    step_down = (factor * contract_first(hidden_all, cotangent_all)).astype(jnp.bfloat16)
    return (out_rows, grad_in, step_gate, step_up, step_down)


def solution(mesh):
    in_specs = (
        P(("sweep", "col"), "row"),
        P("row", "col"),
        P("row", "col"),
        P("col", "row"),
        P(("sweep", "col"), "row"),
        P("sweep"),
    )
    out_specs = (
        P(("sweep", "col"), "row"),
        P(("sweep", "col"), "row"),
        P(("sweep", "row"), "col"),
        P(("sweep", "row"), "col"),
        P(("sweep", "col"), "row"),
    )
    return jax.shard_map(local, mesh=mesh, in_specs=in_specs, out_specs=out_specs, check_vma=False)
```

profile of v0, /device:TPU:40, one launch (start us, length us, event | category | flops | bytes accessed | tf_op | source)
XLA Modules:
  0.0 388.1 jit_solution(322608121071958712)
XLA Ops:
  7.3 99.7 %all-gather.1 = bf16[32,20,512]{2,1,0:T(8,128)(2,1)S(1)} all-gather(bf16[1,20,512]{2,1,0:T(8,128)(2,1)} %bitcast.24), channel_id=1, replica_groups=mesh['sweep'=2,'row'=8,'col'=32] {'col'}, dimensions={0}, use_global_device_ids=true | all-gather | bytes 675840 | tf_op jit(solution)/shard_map/all_gather | solution.py:65
  107.1 1.6 fusion.14
  109.5 55.4 %all-gather = bf16[32,20,512]{2,1,0:T(8,128)(2,1)S(1)} all-gather(bf16[1,20,512]{2,1,0:T(8,128)(2,1)S(1)} %bitcast.25), channel_id=1, replica_groups=mesh['sweep'=2,'row'=8,'col'=32] {'col'}, dimensions={0}, use_global_device_ids=true | all-gather | bytes 675840 | tf_op jit(solution)/shard_map/all_gather | solution.py:46
  165.1 2.3 fusion.12
  167.4 4.6 %all-to-all-start = ((f32[8,80,896]{2,1,0:T(8,128)}), f32[8,80,896]{2,1,0:T(8,128)S(1)}, u32[]{:S(2)}, u32[]{:S(2)}) async-start(f32[8,80,896]{2,1,0:T(8,128)} %bitcast.2), calls=%async_computation | async-start | bytes 4587520 | tf_op jit(solution)/shard_map/all_to_all | solution.py:14
  174.6 26.7 %all-to-all-done = f32[8,80,896]{2,1,0:T(8,128)S(1)} async-done(((f32[8,80,896]{2,1,0:T(8,128)}), f32[8,80,896]{2,1,0:T(8,128)S(1)}, u32[]{:S(2)}, u32[]{:S(2)}) %all-to-all-start) | async-done | bytes 2293792 | tf_op jit(solution)/shard_map/all_to_all | solution.py:14
  203.3 13.3 %all_gather.18 = bf16[640,448]{1,0:T(8,128)(2,1)S(1)} all-gather(bf16[80,448]{1,0:T(8,128)(2,1)S(1)} %get-tuple-element.11), channel_id=1, replica_groups=mesh['sweep'=2,'row'=8,'col'=32] {'row'}, dimensions={0}, use_global_device_ids=true | all-gather | bytes 645120 | tf_op jit(solution)/shard_map/all_gather | solution.py:72
  216.6 13.3 %all_gather.19 = bf16[640,448]{1,0:T(8,128)(2,1)S(1)} all-gather(bf16[80,448]{1,0:T(8,128)(2,1)S(1)} %get-tuple-element.12), channel_id=1, replica_groups=mesh['sweep'=2,'row'=8,'col'=32] {'row'}, dimensions={0}, use_global_device_ids=true | all-gather | bytes 645120 | tf_op jit(solution)/shard_map/all_gather | solution.py:73
  229.9 13.4 %all_gather.16 = bf16[640,448]{1,0:T(8,128)(2,1)S(1)} all-gather(bf16[80,448]{1,0:T(8,128)(2,1)S(1)} %get-tuple-element.13), channel_id=1, replica_groups=mesh['sweep'=2,'row'=8,'col'=32] {'row'}, dimensions={0}, use_global_device_ids=true | all-gather | bytes 645120 | tf_op jit(solution)/shard_map/all_gather | solution.py:56
  243.9 1.9 fusion.5
  245.8 70.9 %fusion.11 = (f32[24,512]{1,0:T(8,128)S(1)}, f32[24,512]{1,0:T(8,128)S(1)}) fusion(f32[640,512]{1,0:T(8,128)S(1)} %fusion.13, f32[640,512]{1,0:T(8,128)} %fusion.5), kind=kCustom, calls=%all-reduce-scatter.2 | all-reduce-scatter fusion | flops 786433 | bytes 2721792
  316.7 5.5 %collective-permute-start.10 = (f32[24,512]{1,0:T(8,128)S(1)}, f32[24,512]{1,0:T(8,128)S(1)}, u32[]{:S(2)}, u32[]{:S(2)}) collective-permute-start(f32[24,512]{1,0:T(8,128)S(1)} %get-tuple-element.8), channel_id=1, source_target_pairs={{0,5},{1,6},{2,7},{3,8},{4,9},{5,10},{6,11},{7,12},{8,13},{9,14},{... | collective-permute-start | bytes 147464
  322.2 4.2 %collective-permute-start.6 = (f32[24,512]{1,0:T(8,128)S(1)}, f32[24,512]{1,0:T(8,128)S(1)}, u32[]{:S(2)}, u32[]{:S(2)}) collective-permute-start(f32[24,512]{1,0:T(8,128)S(1)} %get-tuple-element.8), channel_id=1, source_target_pairs={{0,1},{1,2},{2,3},{3,4},{4,5},{5,6},{6,7},{7,8},{8,9},{9,10},{10,1... | collective-permute-start | bytes 147464
  326.4 2.2 collective-permute-start.7
  328.6 3.1 collective-permute-start.8
  331.7 2.4 convolution_bitcast_fusion
  334.1 3.5 collective-permute-start.11
  338.9 5.2 %collective-permute-start.9 = (f32[24,512]{1,0:T(8,128)S(1)}, f32[24,512]{1,0:T(8,128)S(1)}, u32[]{:S(2)}, u32[]{:S(2)}) collective-permute-start(f32[24,512]{1,0:T(8,128)S(1)} %get-tuple-element.8), channel_id=1, source_target_pairs={{0,4},{1,5},{2,6},{3,7},{4,8},{5,9},{6,10},{7,11},{8,12},{9,13},{1... | collective-permute-start | bytes 147464
  344.1 9.9 %collective-permute-start.5 = (f32[4,512]{1,0:T(4,128)S(1)}, f32[4,512]{1,0:T(4,128)S(1)}, u32[]{:S(2)}, u32[]{:S(2)}) collective-permute-start(f32[4,512]{1,0:T(4,128)S(1)} %slice.20), channel_id=1, source_target_pairs={{0,6},{1,7},{2,8},{3,9},{4,10},{5,11},{6,12},{7,13},{8,14},{9,15},... | collective-permute-start | bytes 24584
  355.4 2.8 collective-permute-start
  358.2 6.5 %collective-permute-start.1 = (f32[24,512]{1,0:T(8,128)S(1)}, f32[24,512]{1,0:T(8,128)S(1)}, u32[]{:S(2)}, u32[]{:S(2)}) collective-permute-start(f32[24,512]{1,0:T(8,128)S(1)} %get-tuple-element.7), channel_id=1, source_target_pairs={{0,2},{1,3},{2,4},{3,5},{4,6},{5,7},{6,8},{7,9},{8,10},{9,11},{10,... | collective-permute-start | bytes 147464
  364.8 5.2 %collective-permute-start.2 = (f32[24,512]{1,0:T(8,128)S(1)}, f32[24,512]{1,0:T(8,128)S(1)}, u32[]{:S(2)}, u32[]{:S(2)}) collective-permute-start(f32[24,512]{1,0:T(8,128)S(1)} %get-tuple-element.7), channel_id=1, source_target_pairs={{0,3},{1,4},{2,5},{3,6},{4,7},{5,8},{6,9},{7,10},{8,11},{9,12},{10... | collective-permute-start | bytes 147464
  370.0 5.0 %collective-permute-start.3 = (f32[24,512]{1,0:T(8,128)S(1)}, f32[24,512]{1,0:T(8,128)S(1)}, u32[]{:S(2)}, u32[]{:S(2)}) collective-permute-start(f32[24,512]{1,0:T(8,128)S(1)} %get-tuple-element.7), channel_id=1, source_target_pairs={{0,4},{1,5},{2,6},{3,7},{4,8},{5,9},{6,10},{7,11},{8,12},{9,13},{1... | collective-permute-start | bytes 147464
  375.9 2.1 collective-permute-start.4
  (53 shorter events, 11.6 us)
Async XLA Ops:
  7.2 99.9 %copy-start = (bf16[448,512]{1,0:T(8,128)(2,1)S(1)}, bf16[448,512]{1,0:T(8,128)(2,1)}, u32[]{:S(2)}) copy-start(bf16[448,512]{1,0:T(8,128)(2,1)} %param.9) | copy-start | bytes 1376260
  7.2 194.9 %reduce-scatter.6.cloned.1.call-start = ((), (), s32[]{:S(2)}) async-start(), calls=%async_computation.2 | async-start | bytes 1474560 | tf_op jit(solution)/shard_map/reduce_scatter | solution.py:67
  107.1 1.6 copy-start.3
  107.1 1.7 copy-start.7
  108.8 56.2 %copy-start.8 = (bf16[512,448]{0,1:T(8,128)(2,1)S(1)}, bf16[512,448]{0,1:T(8,128)(2,1)}, u32[]{:S(2)}) copy-start(bf16[512,448]{0,1:T(8,128)(2,1)} %param.8) | copy-start | bytes 1376260
  165.1 2.3 copy-start.1
  167.4 33.9 %all-to-all-start = ((f32[8,80,896]{2,1,0:T(8,128)}), f32[8,80,896]{2,1,0:T(8,128)S(1)}, u32[]{:S(2)}, u32[]{:S(2)}) async-start(f32[8,80,896]{2,1,0:T(8,128)} %bitcast.2), calls=%async_computation | async-start | bytes 4587520 | tf_op jit(solution)/shard_map/all_to_all | solution.py:14
  216.6 27.2 %copy-start.5 = (bf16[640,448]{1,0:T(8,128)(2,1)}, bf16[640,448]{1,0:T(8,128)(2,1)S(1)}, u32[]{:S(2)}) copy-start(bf16[640,448]{1,0:T(8,128)(2,1)S(1)} %all_gather.18) | copy-start | bytes 1720324
  229.9 13.9 %copy-start.6 = (bf16[640,448]{1,0:T(8,128)(2,1)}, bf16[640,448]{1,0:T(8,128)(2,1)S(1)}, u32[]{:S(2)}) copy-start(bf16[640,448]{1,0:T(8,128)(2,1)S(1)} %all_gather.19) | copy-start | bytes 1720324
  229.9 13.9 %copy-start.2 = (bf16[512,896]{0,1:T(8,128)(2,1)S(1)}, bf16[512,896]{0,1:T(8,128)(2,1)}, u32[]{:S(2)}) copy-start(bf16[512,896]{0,1:T(8,128)(2,1)} %copy-done.1) | copy-start | bytes 2752516
  316.7 27.4 %collective-permute-start.10 = (f32[24,512]{1,0:T(8,128)S(1)}, f32[24,512]{1,0:T(8,128)S(1)}, u32[]{:S(2)}, u32[]{:S(2)}) collective-permute-start(f32[24,512]{1,0:T(8,128)S(1)} %get-tuple-element.8), channel_id=1, source_target_pairs={{0,5},{1,6},{2,7},{3,8},{4,9},{5,10},{6,11},{7,12},{8,13},{9,14},{... | collective-permute-start | bytes 147464
  322.2 33.2 %collective-permute-start.6 = (f32[24,512]{1,0:T(8,128)S(1)}, f32[24,512]{1,0:T(8,128)S(1)}, u32[]{:S(2)}, u32[]{:S(2)}) collective-permute-start(f32[24,512]{1,0:T(8,128)S(1)} %get-tuple-element.8), channel_id=1, source_target_pairs={{0,1},{1,2},{2,3},{3,4},{4,5},{5,6},{6,7},{7,8},{8,9},{9,10},{10,1... | collective-permute-start | bytes 147464
  326.4 31.8 %collective-permute-start.7 = (f32[24,512]{1,0:T(8,128)S(1)}, f32[24,512]{1,0:T(8,128)S(1)}, u32[]{:S(2)}, u32[]{:S(2)}) collective-permute-start(f32[24,512]{1,0:T(8,128)S(1)} %get-tuple-element.8), channel_id=1, source_target_pairs={{0,2},{1,3},{2,4},{3,5},{4,6},{5,7},{6,8},{7,9},{8,10},{9,11},{10,... | collective-permute-start | bytes 147464
  328.6 36.1 %collective-permute-start.8 = (f32[24,512]{1,0:T(8,128)S(1)}, f32[24,512]{1,0:T(8,128)S(1)}, u32[]{:S(2)}, u32[]{:S(2)}) collective-permute-start(f32[24,512]{1,0:T(8,128)S(1)} %get-tuple-element.8), channel_id=1, source_target_pairs={{0,3},{1,4},{2,5},{3,6},{4,7},{5,8},{6,9},{7,10},{8,11},{9,12},{10... | collective-permute-start | bytes 147464
  334.1 20.0 %copy-start.4 = (bf16[640,512]{1,0:T(8,128)(2,1)S(1)}, bf16[640,512]{1,0:T(8,128)(2,1)}, u32[]{:S(2)}) copy-start(bf16[640,512]{1,0:T(8,128)(2,1)} %copy-done.3) | copy-start | bytes 1966084
  334.1 4.8 %collective-permute-start.11 = (f32[4,512]{1,0:T(4,128)S(1)}, f32[4,512]{1,0:T(4,128)S(1)}, u32[]{:S(2)}, u32[]{:S(2)}) collective-permute-start(f32[4,512]{1,0:T(4,128)S(1)} %slice.21), channel_id=1, source_target_pairs={{0,6},{1,7},{2,8},{3,9},{4,10},{5,11},{6,12},{7,13},{8,14},{9,15},... | collective-permute-start | bytes 24584
  338.8 39.3 %copy-start.9 = (bf16[20,512]{1,0:T(8,128)(2,1)S(1)}, bf16[20,512]{1,0:T(8,128)(2,1)}, u32[]{:S(2)}) copy-start(bf16[20,512]{1,0:T(8,128)(2,1)} %param.10) | copy-start | bytes 61444
  338.9 31.0 %collective-permute-start.9 = (f32[24,512]{1,0:T(8,128)S(1)}, f32[24,512]{1,0:T(8,128)S(1)}, u32[]{:S(2)}, u32[]{:S(2)}) collective-permute-start(f32[24,512]{1,0:T(8,128)S(1)} %get-tuple-element.8), channel_id=1, source_target_pairs={{0,4},{1,5},{2,6},{3,7},{4,8},{5,9},{6,10},{7,11},{8,12},{9,13},{1... | collective-permute-start | bytes 147464
  344.1 31.8 %collective-permute-start.5 = (f32[4,512]{1,0:T(4,128)S(1)}, f32[4,512]{1,0:T(4,128)S(1)}, u32[]{:S(2)}, u32[]{:S(2)}) collective-permute-start(f32[4,512]{1,0:T(4,128)S(1)} %slice.20), channel_id=1, source_target_pairs={{0,6},{1,7},{2,8},{3,9},{4,10},{5,11},{6,12},{7,13},{8,14},{9,15},... | collective-permute-start | bytes 24584
  355.4 23.2 %collective-permute-start = (f32[24,512]{1,0:T(8,128)S(1)}, f32[24,512]{1,0:T(8,128)S(1)}, u32[]{:S(2)}, u32[]{:S(2)}) collective-permute-start(f32[24,512]{1,0:T(8,128)S(1)} %get-tuple-element.7), channel_id=1, source_target_pairs={{0,1},{1,2},{2,3},{3,4},{4,5},{5,6},{6,7},{7,8},{8,9},{9,10},{10,1... | collective-permute-start | bytes 147464
  358.2 20.5 %collective-permute-start.1 = (f32[24,512]{1,0:T(8,128)S(1)}, f32[24,512]{1,0:T(8,128)S(1)}, u32[]{:S(2)}, u32[]{:S(2)}) collective-permute-start(f32[24,512]{1,0:T(8,128)S(1)} %get-tuple-element.7), channel_id=1, source_target_pairs={{0,2},{1,3},{2,4},{3,5},{4,6},{5,7},{6,8},{7,9},{8,10},{9,11},{10,... | collective-permute-start | bytes 147464
  364.8 13.9 %collective-permute-start.2 = (f32[24,512]{1,0:T(8,128)S(1)}, f32[24,512]{1,0:T(8,128)S(1)}, u32[]{:S(2)}, u32[]{:S(2)}) collective-permute-start(f32[24,512]{1,0:T(8,128)S(1)} %get-tuple-element.7), channel_id=1, source_target_pairs={{0,3},{1,4},{2,5},{3,6},{4,7},{5,8},{6,9},{7,10},{8,11},{9,12},{10... | collective-permute-start | bytes 147464
  370.0 8.7 %collective-permute-start.3 = (f32[24,512]{1,0:T(8,128)S(1)}, f32[24,512]{1,0:T(8,128)S(1)}, u32[]{:S(2)}, u32[]{:S(2)}) collective-permute-start(f32[24,512]{1,0:T(8,128)S(1)} %get-tuple-element.7), channel_id=1, source_target_pairs={{0,4},{1,5},{2,6},{3,7},{4,8},{5,9},{6,10},{7,11},{8,12},{9,13},{1... | collective-permute-start | bytes 147464
  375.9 3.8 collective-permute-start.4
  (1 other events, 0.7 us)
Sparse Core Ops, SparseCore 0:
  108.9 32.3 reduce-scatter.5
where the time goes:
time: 389 us; the launch traced here: 388 us
  blocking collectives  266 us (68%)
  starting transfers between devices  59.9 us (15%)
  waiting for transfers between devices  28 us (7%)
  between operations  15.7 us (4%)
  matrix products  10 us (3%)
  other arithmetic  4.44 us (1%)
  local copies, waits for them, and re-layouts  3.94 us (1%)
    all_gather x1, blocking collectives, local(): cotangent_all = lax.all_gather(cotangent, 'col', axis=0, tiled=True)  99.7 us
    unnamed x1, blocking collectives  70.9 us
    all_gather x1, blocking collectives, local(): tokens_all = lax.all_gather(tokens, 'col', axis=0, tiled=True)  55.4 us
    unnamed x12, starting transfers between devices  55.2 us
    all_to_all x1, waiting for transfers between devices, summed_on_arrival(): parts = lax.all_to_all(cut_along(value, dim, count), axis, 0, 0, tiled=True)  26.7 us
    all_gather x1, blocking collectives, local(): hidden_all = lax.all_gather(hidden, 'row', axis=0, tiled=True)  13.4 us
    all_gather x1, blocking collectives, local(): lax.all_gather(back_gate, 'row', axis=0, tiled=True)  13.3 us
    all_gather x1, blocking collectives, local(): lax.all_gather(back_up, 'row', axis=0, tiled=True)  13.3 us
  transfers between devices with their start and end apart: 14, of which 3 were waited for; matrix products, arithmetic and copies ran while one was open for 3% of the time, Pallas kernels for 0%

commit v1 on v0

--- a/solution.py
+++ b/solution.py
@@ -43,7 +43,9 @@
 
 
 def local(tokens, w_gate, w_up, w_down, cotangent, step_rate):
-    tokens_all = lax.all_gather(tokens, "col", axis=0, tiled=True)
+    tokens_all = jnp.concatenate(
+        lax.all_to_all(jnp.stack([tokens] * lax.axis_size("col")), "col", 0, 0), axis=0
+    )
     hidden_width = w_gate.shape[1]
     w_both = jnp.concatenate([w_gate, w_up], axis=1)
     picked = tokens_all

time: 389 us -> 425 us (1.093)
  starting transfers between devices: 59.9 us -> 109 us
  blocking collectives: 266 us -> 237 us
  waiting for transfers between devices: 28 us -> 42 us
    all_gather x1 -> x0, blocking collectives: 55.4 us -> none  [local(): tokens_all = lax.all_gather(tokens, 'col', axis=0, tiled=True)]
    all_to_all x0 -> x1, starting transfers between devices: none -> 45.8 us  [local(): lax.all_to_all(jnp.stack([tokens] * lax.axis_size('col')), 'col', 0, 0)]
    all_gather x1, blocking collectives: 99.7 us -> 123 us  [local(): cotangent_all = lax.all_gather(cotangent, 'col', axis=0, tiled=True)]
    reduce_scatter x1, waiting for transfers between devices: 0.01 us -> 10.2 us  [local(): lax.psum_scatter(contract_last(picked, w_down), 'row', scatter_dimension=...]
  transfers between devices with their start and end apart: 14 -> 15, of which waited for: 3 -> 4; matrix products, arithmetic and copies ran while one was open for 3% -> 3% of each run, Pallas kernels for 0% -> 0%
where the time goes in v1:
time: 425 us
  blocking collectives  237 us (56%)
  starting transfers between devices  109 us (26%)
  waiting for transfers between devices  42 us (10%)
  between operations  15.7 us (4%)
  matrix products  9.98 us (2%)
  local copies, waits for them, and re-layouts  6.08 us (1%)
  other arithmetic  4.44 us (1%)
    all_gather x1, blocking collectives, local(): cotangent_all = lax.all_gather(cotangent, 'col', axis=0, tiled=True)  123 us
    unnamed x1, blocking collectives  73.9 us
    unnamed x12, starting transfers between devices  58.7 us
    all_to_all x1, starting transfers between devices, local(): lax.all_to_all(jnp.stack([tokens] * lax.axis_size('col')), 'col', 0, 0)  45.8 us
    all_to_all x1, waiting for transfers between devices, summed_on_arrival(): parts = lax.all_to_all(cut_along(value, dim, count), axis, 0, 0, tiled=True)  30.4 us
    all_gather x1, blocking collectives, local(): hidden_all = lax.all_gather(hidden, 'row', axis=0, tiled=True)  13.4 us
    all_gather x1, blocking collectives, local(): lax.all_gather(back_gate, 'row', axis=0, tiled=True)  13.3 us
    all_gather x1, blocking collectives, local(): lax.all_gather(back_up, 'row', axis=0, tiled=True)  13.3 us
  transfers between devices with their start and end apart: 15, of which 4 were waited for; matrix products, arithmetic and copies ran while one was open for 3% of the time, Pallas kernels for 0%

profile of v1, /device:TPU:40, one launch (start us, length us, event | category | flops | bytes accessed | tf_op | source)
XLA Modules:
  0.0 424.5 jit_solution(2573943568639714799)
XLA Ops:
  8.9 45.8 %all-to-all-start = ((bf16[32,20,512]{2,1,0:T(8,128)(2,1)}), bf16[32,20,512]{2,1,0:T(8,128)(2,1)S(1)}, u32[]{:S(2)}, u32[]{:S(2)}) async-start(bf16[32,20,512]{2,1,0:T(8,128)(2,1)} %stack.2), calls=%async_computation | async-start | bytes 1572864 | tf_op jit(solution)/shard_map/all_to_all | solution.py:47
  54.8 123.3 %all-gather = bf16[32,20,512]{2,1,0:T(8,128)(2,1)S(1)} all-gather(bf16[1,20,512]{2,1,0:T(8,128)(2,1)S(1)} %bitcast.23), channel_id=1, replica_groups=mesh['sweep'=2,'row'=8,'col'=32] {'col'}, dimensions={0}, use_global_device_ids=true | all-gather | bytes 675840 | tf_op jit(solution)/shard_map/all_gather | solution.py:67
  181.2 2.3 fusion.12
  183.5 4.6 %all-to-all-start.1 = ((f32[8,80,896]{2,1,0:T(8,128)}), f32[8,80,896]{2,1,0:T(8,128)S(1)}, u32[]{:S(2)}, u32[]{:S(2)}) async-start(f32[8,80,896]{2,1,0:T(8,128)} %bitcast.1), calls=%async_computation.1 | async-start | bytes 4587520 | tf_op jit(solution)/shard_map/all_to_all | solution.py:14
  190.7 30.4 %all-to-all-done.1 = f32[8,80,896]{2,1,0:T(8,128)S(1)} async-done(((f32[8,80,896]{2,1,0:T(8,128)}), f32[8,80,896]{2,1,0:T(8,128)S(1)}, u32[]{:S(2)}, u32[]{:S(2)}) %all-to-all-start.1) | async-done | bytes 2293792 | tf_op jit(solution)/shard_map/all_to_all | solution.py:14
  221.9 10.2 %reduce-scatter.6.cloned.1.call-done = f32[80,448]{1,0:T(8,128)} async-done(((f32[640,448]{1,0:T(8,128)}), f32[80,448]{1,0:T(8,128)}) %reduce-scatter.6.cloned.1.call-update) | async-done | bytes 143376 | tf_op jit(solution)/shard_map/reduce_scatter | solution.py:69
  233.3 13.3 %all_gather.14 = bf16[640,448]{1,0:T(8,128)(2,1)S(1)} all-gather(bf16[80,448]{1,0:T(8,128)(2,1)S(1)} %get-tuple-element.11), channel_id=1, replica_groups=mesh['sweep'=2,'row'=8,'col'=32] {'row'}, dimensions={0}, use_global_device_ids=true | all-gather | bytes 645120 | tf_op jit(solution)/shard_map/all_gather | solution.py:74
  246.6 13.3 %all_gather.15 = bf16[640,448]{1,0:T(8,128)(2,1)S(1)} all-gather(bf16[80,448]{1,0:T(8,128)(2,1)S(1)} %get-tuple-element.12), channel_id=1, replica_groups=mesh['sweep'=2,'row'=8,'col'=32] {'row'}, dimensions={0}, use_global_device_ids=true | all-gather | bytes 645120 | tf_op jit(solution)/shard_map/all_gather | solution.py:75
  259.9 13.4 %all_gather.12 = bf16[640,448]{1,0:T(8,128)(2,1)S(1)} all-gather(bf16[80,448]{1,0:T(8,128)(2,1)S(1)} %get-tuple-element.13), channel_id=1, replica_groups=mesh['sweep'=2,'row'=8,'col'=32] {'row'}, dimensions={0}, use_global_device_ids=true | all-gather | bytes 645120 | tf_op jit(solution)/shard_map/all_gather | solution.py:58
  273.9 1.9 fusion.5
  275.8 73.9 %fusion.11 = (f32[24,512]{1,0:T(8,128)S(1)}, f32[24,512]{1,0:T(8,128)S(1)}) fusion(f32[640,512]{1,0:T(8,128)S(1)} %fusion.13, f32[640,512]{1,0:T(8,128)} %fusion.5), kind=kCustom, calls=%all-reduce-scatter.2 | all-reduce-scatter fusion | flops 786433 | bytes 2721792
  349.7 6.0 %collective-permute-start.10 = (f32[24,512]{1,0:T(8,128)S(1)}, f32[24,512]{1,0:T(8,128)S(1)}, u32[]{:S(2)}, u32[]{:S(2)}) collective-permute-start(f32[24,512]{1,0:T(8,128)S(1)} %get-tuple-element.8), channel_id=1, source_target_pairs={{0,5},{1,6},{2,7},{3,8},{4,9},{5,10},{6,11},{7,12},{8,13},{9,14},{... | collective-permute-start | bytes 147464
  355.8 3.4 collective-permute-start.6
  359.2 5.1 %collective-permute-start.7 = (f32[24,512]{1,0:T(8,128)S(1)}, f32[24,512]{1,0:T(8,128)S(1)}, u32[]{:S(2)}, u32[]{:S(2)}) collective-permute-start(f32[24,512]{1,0:T(8,128)S(1)} %get-tuple-element.8), channel_id=1, source_target_pairs={{0,2},{1,3},{2,4},{3,5},{4,6},{5,7},{6,8},{7,9},{8,10},{9,11},{10,... | collective-permute-start | bytes 147464
  364.3 6.0 %collective-permute-start.8 = (f32[24,512]{1,0:T(8,128)S(1)}, f32[24,512]{1,0:T(8,128)S(1)}, u32[]{:S(2)}, u32[]{:S(2)}) collective-permute-start(f32[24,512]{1,0:T(8,128)S(1)} %get-tuple-element.8), channel_id=1, source_target_pairs={{0,3},{1,4},{2,5},{3,6},{4,7},{5,8},{6,9},{7,10},{8,11},{9,12},{10... | collective-permute-start | bytes 147464
  370.3 2.4 convolution_bitcast_fusion
  372.7 10.8 %collective-permute-start.11 = (f32[4,512]{1,0:T(4,128)S(1)}, f32[4,512]{1,0:T(4,128)S(1)}, u32[]{:S(2)}, u32[]{:S(2)}) collective-permute-start(f32[4,512]{1,0:T(4,128)S(1)} %slice.21), channel_id=1, source_target_pairs={{0,6},{1,7},{2,8},{3,9},{4,10},{5,11},{6,12},{7,13},{8,14},{9,15},... | collective-permute-start | bytes 24584
  384.8 3.5 collective-permute-start.9
  388.4 10.1 %collective-permute-start.5 = (f32[4,512]{1,0:T(4,128)S(1)}, f32[4,512]{1,0:T(4,128)S(1)}, u32[]{:S(2)}, u32[]{:S(2)}) collective-permute-start(f32[4,512]{1,0:T(4,128)S(1)} %slice.20), channel_id=1, source_target_pairs={{0,6},{1,7},{2,8},{3,9},{4,10},{5,11},{6,12},{7,13},{8,14},{9,15},... | collective-permute-start | bytes 24584
  399.8 1.8 collective-permute-start
  401.6 3.9 collective-permute-start.1
  405.5 3.5 collective-permute-start.2
  409.1 2.3 collective-permute-start.3
  412.2 2.2 collective-permute-start.4
  (53 shorter events, 15.3 us)
Async XLA Ops:
  7.2 171.1 %copy-start = (bf16[448,512]{1,0:T(8,128)(2,1)S(1)}, bf16[448,512]{1,0:T(8,128)(2,1)}, u32[]{:S(2)}) copy-start(bf16[448,512]{1,0:T(8,128)(2,1)} %param.9) | copy-start | bytes 1376260
  7.2 47.6 %copy-start.8 = (bf16[20,512]{1,0:T(8,128)(2,1)S(1)}, bf16[20,512]{1,0:T(8,128)(2,1)}, u32[]{:S(2)}) copy-start(bf16[20,512]{1,0:T(8,128)(2,1)} %param.10) | copy-start | bytes 61444
  8.9 172.1 %all-to-all-start = ((bf16[32,20,512]{2,1,0:T(8,128)(2,1)}), bf16[32,20,512]{2,1,0:T(8,128)(2,1)S(1)}, u32[]{:S(2)}, u32[]{:S(2)}) async-start(bf16[32,20,512]{2,1,0:T(8,128)(2,1)} %stack.2), calls=%async_computation | async-start | bytes 1572864 | tf_op jit(solution)/shard_map/all_to_all | solution.py:47
  54.7 177.4 %reduce-scatter.6.cloned.1.call-start = ((), (), s32[]{:S(2)}) async-start(), calls=%async_computation.3 | async-start | bytes 1474560 | tf_op jit(solution)/shard_map/reduce_scatter | solution.py:69
  178.3 1.7 copy-start.3
  181.1 2.4 copy-start.1
  183.5 37.6 %all-to-all-start.1 = ((f32[8,80,896]{2,1,0:T(8,128)}), f32[8,80,896]{2,1,0:T(8,128)S(1)}, u32[]{:S(2)}, u32[]{:S(2)}) async-start(f32[8,80,896]{2,1,0:T(8,128)} %bitcast.1), calls=%async_computation.1 | async-start | bytes 4587520 | tf_op jit(solution)/shard_map/all_to_all | solution.py:14
  246.6 27.2 %copy-start.5 = (bf16[640,448]{1,0:T(8,128)(2,1)}, bf16[640,448]{1,0:T(8,128)(2,1)S(1)}, u32[]{:S(2)}) copy-start(bf16[640,448]{1,0:T(8,128)(2,1)S(1)} %all_gather.14) | copy-start | bytes 1720324
  259.9 13.9 %copy-start.6 = (bf16[640,448]{1,0:T(8,128)(2,1)}, bf16[640,448]{1,0:T(8,128)(2,1)S(1)}, u32[]{:S(2)}) copy-start(bf16[640,448]{1,0:T(8,128)(2,1)S(1)} %all_gather.15) | copy-start | bytes 1720324
  259.9 13.9 %copy-start.2 = (bf16[512,896]{0,1:T(8,128)(2,1)S(1)}, bf16[512,896]{0,1:T(8,128)(2,1)}, u32[]{:S(2)}) copy-start(bf16[512,896]{0,1:T(8,128)(2,1)} %copy-done.1) | copy-start | bytes 2752516
  349.7 38.7 %collective-permute-start.10 = (f32[24,512]{1,0:T(8,128)S(1)}, f32[24,512]{1,0:T(8,128)S(1)}, u32[]{:S(2)}, u32[]{:S(2)}) collective-permute-start(f32[24,512]{1,0:T(8,128)S(1)} %get-tuple-element.8), channel_id=1, source_target_pairs={{0,5},{1,6},{2,7},{3,8},{4,9},{5,10},{6,11},{7,12},{8,13},{9,14},{... | collective-permute-start | bytes 147464
  355.8 44.0 %collective-permute-start.6 = (f32[24,512]{1,0:T(8,128)S(1)}, f32[24,512]{1,0:T(8,128)S(1)}, u32[]{:S(2)}, u32[]{:S(2)}) collective-permute-start(f32[24,512]{1,0:T(8,128)S(1)} %get-tuple-element.8), channel_id=1, source_target_pairs={{0,1},{1,2},{2,3},{3,4},{4,5},{5,6},{6,7},{7,8},{8,9},{9,10},{10,1... | collective-permute-start | bytes 147464
  359.2 42.4 %collective-permute-start.7 = (f32[24,512]{1,0:T(8,128)S(1)}, f32[24,512]{1,0:T(8,128)S(1)}, u32[]{:S(2)}, u32[]{:S(2)}) collective-permute-start(f32[24,512]{1,0:T(8,128)S(1)} %get-tuple-element.8), channel_id=1, source_target_pairs={{0,2},{1,3},{2,4},{3,5},{4,6},{5,7},{6,8},{7,9},{8,10},{9,11},{10,... | collective-permute-start | bytes 147464
  364.3 41.2 %collective-permute-start.8 = (f32[24,512]{1,0:T(8,128)S(1)}, f32[24,512]{1,0:T(8,128)S(1)}, u32[]{:S(2)}, u32[]{:S(2)}) collective-permute-start(f32[24,512]{1,0:T(8,128)S(1)} %get-tuple-element.8), channel_id=1, source_target_pairs={{0,3},{1,4},{2,5},{3,6},{4,7},{5,8},{6,9},{7,10},{8,11},{9,12},{10... | collective-permute-start | bytes 147464
  372.7 25.8 %copy-start.4 = (bf16[640,512]{1,0:T(8,128)(2,1)S(1)}, bf16[640,512]{1,0:T(8,128)(2,1)}, u32[]{:S(2)}) copy-start(bf16[640,512]{1,0:T(8,128)(2,1)} %copy-done.3) | copy-start | bytes 1966084
  372.7 12.1 %collective-permute-start.11 = (f32[4,512]{1,0:T(4,128)S(1)}, f32[4,512]{1,0:T(4,128)S(1)}, u32[]{:S(2)}, u32[]{:S(2)}) collective-permute-start(f32[4,512]{1,0:T(4,128)S(1)} %slice.21), channel_id=1, source_target_pairs={{0,6},{1,7},{2,8},{3,9},{4,10},{5,11},{6,12},{7,13},{8,14},{9,15},... | collective-permute-start | bytes 24584
  384.7 32.4 %copy-start.9 = (bf16[20,512]{1,0:T(8,128)(2,1)S(1)}, bf16[20,512]{1,0:T(8,128)(2,1)}, u32[]{:S(2)}) copy-start(bf16[20,512]{1,0:T(8,128)(2,1)} %param.6) | copy-start | bytes 61444
  384.8 24.2 %collective-permute-start.9 = (f32[24,512]{1,0:T(8,128)S(1)}, f32[24,512]{1,0:T(8,128)S(1)}, u32[]{:S(2)}, u32[]{:S(2)}) collective-permute-start(f32[24,512]{1,0:T(8,128)S(1)} %get-tuple-element.8), channel_id=1, source_target_pairs={{0,4},{1,5},{2,6},{3,7},{4,8},{5,9},{6,10},{7,11},{8,12},{9,13},{1... | collective-permute-start | bytes 147464
  388.4 23.9 %collective-permute-start.5 = (f32[4,512]{1,0:T(4,128)S(1)}, f32[4,512]{1,0:T(4,128)S(1)}, u32[]{:S(2)}, u32[]{:S(2)}) collective-permute-start(f32[4,512]{1,0:T(4,128)S(1)} %slice.20), channel_id=1, source_target_pairs={{0,6},{1,7},{2,8},{3,9},{4,10},{5,11},{6,12},{7,13},{8,14},{9,15},... | collective-permute-start | bytes 24584
  399.8 15.3 %collective-permute-start = (f32[24,512]{1,0:T(8,128)S(1)}, f32[24,512]{1,0:T(8,128)S(1)}, u32[]{:S(2)}, u32[]{:S(2)}) collective-permute-start(f32[24,512]{1,0:T(8,128)S(1)} %get-tuple-element.7), channel_id=1, source_target_pairs={{0,1},{1,2},{2,3},{3,4},{4,5},{5,6},{6,7},{7,8},{8,9},{9,10},{10,1... | collective-permute-start | bytes 147464
  401.6 13.5 %collective-permute-start.1 = (f32[24,512]{1,0:T(8,128)S(1)}, f32[24,512]{1,0:T(8,128)S(1)}, u32[]{:S(2)}, u32[]{:S(2)}) collective-permute-start(f32[24,512]{1,0:T(8,128)S(1)} %get-tuple-element.7), channel_id=1, source_target_pairs={{0,2},{1,3},{2,4},{3,5},{4,6},{5,7},{6,8},{7,9},{8,10},{9,11},{10,... | collective-permute-start | bytes 147464
  405.5 9.6 %collective-permute-start.2 = (f32[24,512]{1,0:T(8,128)S(1)}, f32[24,512]{1,0:T(8,128)S(1)}, u32[]{:S(2)}, u32[]{:S(2)}) collective-permute-start(f32[24,512]{1,0:T(8,128)S(1)} %get-tuple-element.7), channel_id=1, source_target_pairs={{0,3},{1,4},{2,5},{3,6},{4,7},{5,8},{6,9},{7,10},{8,11},{9,12},{10... | collective-permute-start | bytes 147464
  409.1 6.0 %collective-permute-start.3 = (f32[24,512]{1,0:T(8,128)S(1)}, f32[24,512]{1,0:T(8,128)S(1)}, u32[]{:S(2)}, u32[]{:S(2)}) collective-permute-start(f32[24,512]{1,0:T(8,128)S(1)} %get-tuple-element.7), channel_id=1, source_target_pairs={{0,4},{1,5},{2,6},{3,7},{4,8},{5,9},{6,10},{7,11},{8,12},{9,13},{1... | collective-permute-start | bytes 147464
  412.2 4.0 collective-permute-start.4
  (1 other events, 1.7 us)
Sparse Core Ops, SparseCore 0:
  180.1 52.0 reduce-scatter.5
